TPU v7x, 32 devices: a whole 2x2x4 slice. The times are simulated.
32 devices in a mesh: shot: 4 (over y, core), space: 8 (over z, x).
Axes of the slice: x: 2, y: 2, z: 4, core: 2. Of those that a mesh axis runs over, the one named last changes fastest.
Arguments:
- adjoint_now: float32 [4, 128, 64, 512], P('shot', 'space'), may hold values from -6 to 6
- adjoint_later: float32 [4, 128, 64, 512], P('shot', 'space'), may hold values from -6 to 6
- courant: float32 [128, 64, 512], P('space'), may hold values from 0.05 to 0.2
- checkpoint_codes: int32 [4, 6, 128, 64, 128], P('shot', None, 'space'), may hold values from -2147483648 to 2147483646
- scale_index: int32 [4, 6, 128, 256], P('shot', None, 'space'), may hold values from 0 to 63
- scale_table: float32 [64], replicated, may hold values from 0.001 to 0.01
- receiver_cell: int32 [4, 2048], P('shot', 'space'), may hold values from 0 to 4194303, as said below
- observed: float32 [4, 4, 2048], P('shot', None, 'space'), may hold values from -12 to 12
- source_cell: int32 [4, 3], P('shot'), may hold values from 0 to 511, as said below
Outputs:
- gradient: float32 [128, 64, 512], P('space', 'shot')
- adjoint_first: float32 [4, 128, 64, 512], P('shot', 'space')
- adjoint_second: float32 [4, 128, 64, 512], P('shot', 'space')
- misfit: float32 [], replicated
Inputs may be any that keep to these rules, and one draw needn't show every extreme that they name: `receiver_cell`: for every r, entries r * 256 to (r + 1) * 256 - 1 of each shot's row are flat indices (z * 64 + y) * 512 + x of cells with r * 16 <= z < (r + 1) * 16. `source_cell`: column 0 is a z index below 128, column 1 a y index below 64, column 2 an x index below 512.
All inputs are finite; a program needn't handle non-finite values.
Results may differ from a plain program's by a relative error of at most 0.0001.
Values sent between devices are 32-bit elements; how exact they have to be, the bound alone decides.
A program may use at most 128 MiB of HBM per device.

v0:
```python
import jax
import jax.numpy as jnp
from jax import lax
from jax.sharding import PartitionSpec as P

ITERS = 4
QBLOCK = 128
MUTE = 8
COEFFS = (-205.0 / 72.0, 8.0 / 5.0, -1.0 / 5.0, 8.0 / 315.0, -1.0 / 560.0)


def with_halo(block, sides, width):
    for axis, dim in sides:
        count = lax.axis_size(axis)
        forward = [(i, i + 1) for i in range(count - 1)]
        backward = [(target, source) for source, target in forward]
        low = lax.ppermute(
            lax.slice_in_dim(block, block.shape[dim] - width, None, axis=dim), axis, forward
        )
        high = lax.ppermute(lax.slice_in_dim(block, 0, width, axis=dim), axis, backward)
        block = jnp.concatenate([low, block, high], axis=dim)
    return block


def decode(words, index, table):
    planes = [jnp.bitwise_and(jnp.right_shift(words, 8 * m), 255) for m in range(4)]
    codes = jnp.concatenate(planes, axis=-1)
    centred = (codes - 128).astype(jnp.float32)
    depth, rows, cols = centred.shape
    onehot = index[..., None] == jnp.arange(table.shape[0], dtype=jnp.int32)
    scale = jnp.sum(jnp.where(onehot, table, 0.0), axis=-1)
    blocks = centred.reshape(depth, rows, cols // QBLOCK, QBLOCK) * scale.reshape(
        depth, rows, cols // QBLOCK, 1
    )
    return blocks.reshape(depth, rows, cols)


def laplace(field):
    depth, rows, cols = field.shape
    deep = with_halo(field, (("space", 0),), 4)
    flat = jnp.pad(field, ((0, 0), (4, 4), (4, 4)))
    total = 3.0 * COEFFS[0] * field
    for step in range(1, 5):
        total = total + COEFFS[step] * (
            deep[4 + step : 4 + step + depth] + deep[4 - step : 4 - step + depth]
        )
        total = total + COEFFS[step] * (
            flat[:, 4 + step : 4 + step + rows, 4 : 4 + cols]
            + flat[:, 4 - step : 4 - step + rows, 4 : 4 + cols]
        )
        total = total + COEFFS[step] * (
            flat[:, 4 : 4 + rows, 4 + step : 4 + step + cols]
            + flat[:, 4 : 4 + rows, 4 - step : 4 - step + cols]
        )
    return total


def body(
    adjoint_now,
    adjoint_later,
    courant,
    checkpoint_codes,
    scale_index,
    scale_table,
    receiver_cell,
    observed,
    source_cell,
):
    now = adjoint_now[0]
    later = adjoint_later[0]
    depth, rows, cols = now.shape
    first_z = lax.axis_index("space") * depth
    cells = receiver_cell[0] - first_z * (rows * cols)
    fields = [
        decode(checkpoint_codes[0, level], scale_index[0, level], scale_table)
        for level in range(ITERS + 2)
    ]
    image = jnp.zeros((depth, rows, cols), jnp.float32)
    misfit_part = jnp.zeros((), jnp.float32)
    for step in range(ITERS):
        level = ITERS - step
        synthetic = jnp.take(fields[level].reshape(-1), cells)
        residual = synthetic - observed[0, level - 1]
        misfit_part = misfit_part + jnp.sum(residual * residual)
        image = image + now * (fields[level + 1] - 2.0 * fields[level] + fields[level - 1])
        stepped = 2.0 * now - later + courant * laplace(now)
        stepped = stepped.reshape(-1).at[cells].add(residual).reshape(depth, rows, cols)
        later = now
        now = stepped
    source = source_cell[0]
    zpos = (first_z + jnp.arange(depth, dtype=jnp.int32)).reshape(depth, 1, 1)
    ypos = jnp.arange(rows, dtype=jnp.int32).reshape(1, rows, 1)
    xpos = jnp.arange(cols, dtype=jnp.int32).reshape(1, 1, cols)
    dist = ((zpos - source[0]) ** 2 + (ypos - source[1]) ** 2 + (xpos - source[2]) ** 2).astype(
        jnp.float32
    )
    muted = image * (1.0 - jnp.exp(-dist / (2.0 * MUTE * MUTE)))
    gradient = lax.psum_scatter(muted, "shot", scatter_dimension=1, tiled=True)
    count = lax.axis_size("shot") * ITERS * receiver_cell.shape[1] * lax.axis_size("space")
    misfit = 0.5 * lax.psum(misfit_part, ("shot", "space")) / count
    return (gradient, now[None], later[None], misfit)


def solution(mesh):
    placed = (
        P("shot", "space", None, None),
        P("shot", "space", None, None),
        P("space", None, None),
        P("shot", None, "space", None, None),
        P("shot", None, "space", None),
        P(),
        P("shot", "space"),
        P("shot", None, "space"),
        P("shot", None),
    )
    return jax.shard_map(
        body,
        mesh=mesh,
        in_specs=placed,
        out_specs=(
            P("space", "shot", None),
            P("shot", "space", None, None),
            P("shot", "space", None, None),
            P(),
        ),
        check_vma=False,
    )
```

profile of v0, /device:TPU:0, one launch (start us, length us, event | category | flops | bytes accessed | tf_op | source)
XLA Modules:
  0.0 308.4 jit_solution(9114764034815318383)
XLA Ops:
  10.8 6.3 %collective-permute-start.1 = (f32[4,64,512]{2,1,0:T(8,128)}, f32[4,64,512]{2,1,0:T(8,128)}, u32[]{:S(2)}, u32[]{:S(2)}) collective-permute-start(f32[4,64,512]{2,1,0:T(8,128)} %get-tuple-element.59), channel_id=1, source_target_pairs={{0,1},{1,2},{2,3},{3,4},{4,5},{5,6},{6,7},{8,9},{9,10},{10,11},{11... | collective-permute-start | bytes 1572872 | tf_op jit(solution)/shard_map/ppermute | solution.py:17
  17.1 3.3 %and_bitcast_fusion.7 = (s32[16,64,1,128]{3,1,0,2:T(8,128)}, s32[16,64,1,128]{3,1,0,2:T(8,128)}, s32[16,64,1,128]{3,1,0,2:T(8,128)}, s32[16,64,1,128]{3,1,0,2:T(8,128)}, s32[16,64,1,128]{3,1,0,2:T(8,128)S(1)}) fusion(s32[1,6,16,64,128]{4,3,2,1,0:T(8,128)} %param.14), kind=kLoop, calls=%fused_computation.304 | loop fusion | flops 1310720 | bytes 5242880 | tf_op jit(solution)/shard_map/and | solution.py:26
  20.4 3.7 %and_bitcast_fusion.23 = (s32[16,64,1,128]{3,1,0,2:T(8,128)S(1)}, s32[16,64,1,128]{3,1,0,2:T(8,128)}, s32[16,64,1,128]{3,1,0,2:T(8,128)}, s32[16,64,1,128]{3,1,0...) fusion(s32[1,6,16,64,128]{4,3,2,1,0:T(8,128)S(1)} %copy-done.11), kind=kLoop, calls=%fused_computation.322 | loop fusion | flops 4980736 | bytes 13107200 | tf_op jit(solution)/shard_map/and | solution.py:26
  26.5 3.9 %fusion.162 = (f32[16,64,4,128]{3,1,0,2:T(8,128)S(1)}, f32[16,64,4,128]{3,1,0,2:T(8,128)S(1)}) fusion(s32[16,64,1,128]{3,1,0,2:T(8,128)} %get-tuple-element.27, s32[16,64,1,128]{3,1,0,2:T(8,128)} %get-tuple-element.26, s32[16,64,1,128]{3,1,0,2:T(8,128)} %get-tuple-element.25, s32[16,64,1,128]{3,1,0,2:T(8,128)} %get-tuple-element.43, ...), kind=kLoop, calls=%fused_computation.270 | loop fusion | flops 6291456 | bytes 8421376 | tf_op jit(solution)/shard_map/mul | solution.py:32
  38.6 3.4 %gather_fusion = f32[256]{0:T(256)S(1)} fusion(f32[524288]{0:T(1024)} %bitcast.181, s32[1024]{0:T(1024)S(1)} %pad_clamp_fusion), kind=kCustom, calls=%fused_computation.clone | custom fusion | bytes 3072 | tf_op jit(solution)/shard_map/jit(_take)/gather | solution.py:82
  42.0 3.5 %gather_fusion.1 = f32[256]{0:T(256)S(1)} fusion(f32[524288]{0:T(1024)} %bitcast.182, s32[1024]{0:T(1024)S(1)} %pad_clamp_fusion), kind=kCustom, calls=%fused_computation.1.clone | custom fusion | bytes 3072 | tf_op jit(solution)/shard_map/jit(_take)/gather | solution.py:82
  48.2 3.5 %gather_fusion.2 = f32[256]{0:T(256)S(1)} fusion(f32[524288]{0:T(1024)} %bitcast.184, s32[1024]{0:T(1024)S(1)} %pad_clamp_fusion), kind=kCustom, calls=%fused_computation.2.clone | custom fusion | bytes 3072 | tf_op jit(solution)/shard_map/jit(_take)/gather | solution.py:82
  51.7 4.5 %copy.51 = f32[16,64,4,128]{3,2,1,0:T(4,128)} copy(f32[16,64,4,128]{3,1,0,2:T(8,128)} %get-tuple-element.84) | data formatting | bytes 4194304 | tf_op jit(solution)/shard_map/mul | solution.py:32
  56.2 3.5 %gather_fusion.3 = f32[256]{0:T(256)S(1)} fusion(f32[524288]{0:T(1024)} %bitcast.183, s32[1024]{0:T(1024)S(1)} %pad_clamp_fusion), kind=kCustom, calls=%fused_computation.3.clone | custom fusion | bytes 3072 | tf_op jit(solution)/shard_map/jit(_take)/gather | solution.py:82
  60.3 29.2 %fusion.10 = f32[16,64,512]{2,1,0:T(8,128)S(1)} fusion(f32[16,64,512]{2,1,0:T(8,128)S(1)} %copy-done.2, f32[16,64,512]{2,1,0:T(8,128)} %bitcast.173, f32[4,64,512]{2,1,0:T(8,128)} %collective-permute-done.1, f32[4,64,512]{2,1,0:T(8,128)} %collective-permute-done, f32[1,16,64,512]{3,2,1,0:T(8,128)} %param.12), kind=kLoop, calls=%fused_computation.94 | loop fusion | flops 25690112 | bytes 9437184 | tf_op jit(solution)/shard_map/add | solution.py:86
  90.1 2.9 scatter_fusion
  96.1 4.8 %collective-permute-start.3 = (f32[4,64,512]{2,1,0:T(8,128)}, f32[4,64,512]{2,1,0:T(8,128)}, u32[]{:S(2)}, u32[]{:S(2)}) collective-permute-start(f32[4,64,512]{2,1,0:T(8,128)} %slice.517), channel_id=1, source_target_pairs={{0,1},{1,2},{2,3},{3,4},{4,5},{5,6},{6,7},{8,9},{9,10},{10,11},{11... | collective-permute-start | bytes 1572872 | tf_op jit(solution)/shard_map/ppermute | solution.py:17
  105.9 16.4 %collective-permute-done.3 = f32[4,64,512]{2,1,0:T(8,128)} collective-permute-done((f32[4,64,512]{2,1,0:T(8,128)}, f32[4,64,512]{2,1,0:T(8,128)}, u32[]{:S(2)}, u32[]{:S(2)}) %collective-permute-start.3) | collective-permute-done | bytes 524320 | tf_op jit(solution)/shard_map/ppermute | solution.py:17
  125.8 4.9 %fusion.56 = f32[16,64,512]{2,1,0:T(8,128)S(1)} fusion(f32[16,64,512]{2,1,0:T(8,128)S(1)} %copy-done.3, f32[16,64,512]{2,1,0:T(8,128)S(1)} %reshape.603, f32[20,64,512]{2,1,0:T(8,128)S(1)} %get-tuple-element.57, f32[20,64,512]{2,1,0:T(8,128)S(1)} %constant_dynamic-update-slice_fusion, f32[1,16,64,512]{3,2,1,0:T(8,128)S(1)} %copy-done.6), kind=kLoop, calls=%fused_computation.140 | loop fusion | flops 21495808 | bytes 25165824 | tf_op jit(solution)/shard_map/add | solution.py:86
  132.5 4.8 %scatter_fusion.1 = f32[524288]{0:T(1024)} fusion(f32[524288]{0:T(1024)} %bitcast.175, s32[256]{0:T(256)S(1)} %bitcast.192, f32[256]{0:T(256)S(1)} %get-tuple-element.71), kind=kCustom, calls=%fused_computation.5 | custom fusion | flops 256 | bytes 4096 | tf_op jit(solution)/shard_map/scatter-add | solution.py:87
  141.5 5.2 %collective-permute-start.5 = (f32[4,64,512]{2,1,0:T(8,128)}, f32[4,64,512]{2,1,0:T(8,128)}, u32[]{:S(2)}, u32[]{:S(2)}) collective-permute-start(f32[4,64,512]{2,1,0:T(8,128)} %slice.548), channel_id=1, source_target_pairs={{0,1},{1,2},{2,3},{3,4},{4,5},{5,6},{6,7},{8,9},{9,10},{10,11},{11... | collective-permute-start | bytes 1572872 | tf_op jit(solution)/shard_map/ppermute | solution.py:17
  155.6 11.6 %collective-permute-done.5 = f32[4,64,512]{2,1,0:T(8,128)} collective-permute-done((f32[4,64,512]{2,1,0:T(8,128)}, f32[4,64,512]{2,1,0:T(8,128)}, u32[]{:S(2)}, u32[]{:S(2)}) %collective-permute-start.5) | collective-permute-done | bytes 524320 | tf_op jit(solution)/shard_map/ppermute | solution.py:17
  171.6 5.0 %fusion.85 = f32[16,64,512]{2,1,0:T(8,128)S(1)} fusion(f32[16,64,512]{2,1,0:T(8,128)S(1)} %copy-done.4, f32[16,64,512]{2,1,0:T(8,128)S(1)} %copy-done, f32[20,64,512]{2,1,0:T(8,128)S(1)} %get-tuple-element.53, f32[20,64,512]{2,1,0:T(8,128)S(1)} %constant_dynamic-update-slice_fusion.4, f32[16,64,512]{2,1,0:T(8,128)S(1)} %reshape.603), kind=kLoop, calls=%fused_computation.169 | loop fusion | flops 21495808 | bytes 25165824 | tf_op jit(solution)/shard_map/add | solution.py:86
  178.5 4.8 %scatter_fusion.2 = f32[524288]{0:T(1024)} fusion(f32[524288]{0:T(1024)} %bitcast.172, s32[256]{0:T(256)S(1)} %bitcast.193, f32[256]{0:T(256)S(1)} %get-tuple-element.73), kind=kCustom, calls=%fused_computation.6 | custom fusion | flops 256 | bytes 4096 | tf_op jit(solution)/shard_map/scatter-add | solution.py:87
  187.4 5.2 %collective-permute-start.7 = (f32[4,64,512]{2,1,0:T(8,128)}, f32[4,64,512]{2,1,0:T(8,128)}, u32[]{:S(2)}, u32[]{:S(2)}) collective-permute-start(f32[4,64,512]{2,1,0:T(8,128)} %slice.582), channel_id=1, source_target_pairs={{0,1},{1,2},{2,3},{3,4},{4,5},{5,6},{6,7},{8,9},{9,10},{10,11},{11... | collective-permute-start | bytes 1572872 | tf_op jit(solution)/shard_map/ppermute | solution.py:17
  192.7 5.2 %fusion.160 = (f32[4,16,8,8,128]{4,3,2,1,0:T(8,128)}, f32[4,16,8,8,128]{4,3,2,1,0:T(8,128)}) fusion(s32[16,64,1,128]{3,1,0,2:T(8,128)} %get-tuple-element.24, s32[16,64,1,128]{3,1,0,2:T(8,128)} %get-tuple-element.23, s32[16,64,1,128]{3,1,0,2:T(8,128)} %get-tuple-element.22, s32[16,64,1,128]{3,1,0,2:T(8,128)S(1)} %get-tuple-element.21, ...), kind=kLoop, calls=%fused_computation.267 | loop fusion | flops 6291456 | bytes 8421376
  202.1 9.6 %constant_dynamic-update-slice_fusion.9 = (f32[20,64,512]{2,1,0:T(8,128)}, f32[20,64,512]{2,1,0:T(8,128)S(1)}, f32[16,64,512]{2,1,0:T(8,128)}) fusion(f32[16,64,512]{2,1,0:T(8,128)} %reshape.607, f32[20,64,512]{2,1,0:T(8,128)S(1)} %constant_dynamic-update-slice_fusion.11, s32[512]{0:T(512)S(1)} %subtract_multiply_fusion, ...), kind=kLoop, calls=%fused_computation.332 | loop fusion | flops 13107199 | bytes 27273216
  218.3 46.7 %psum.7 = f32[]{:T(128)} all-reduce(f32[]{:T(128)S(6)} %add.560), channel_id=1, replica_groups=mesh['shot'=4,'space'=8] {'shot','space'}, use_global_device_ids=true, to_apply=%region_15.17 | all-reduce | flops 1 | bytes 8 | tf_op jit(solution)/shard_map/psum | solution.py:100
  269.4 26.3 %fusion.114 = f32[16,64,512]{2,1,0:T(8,128)S(1)} fusion(f32[16,64,512]{2,1,0:T(8,128)} %param.13, f32[16,64,512]{2,1,0:T(8,128)} %reshape.607, f32[20,64,512]{2,1,0:T(8,128)} %copy-done.5, f32[20,64,512]{2,1,0:T(8,128)} %constant_dynamic-update-slice_fusion.8, f32[16,64,512]{2,1,0:T(8,128)S(1)} %copy-done.1), kind=kLoop, calls=%fused_computation.198 | loop fusion | flops 21495808 | bytes 25165824 | tf_op jit(solution)/shard_map/add | solution.py:86
  (121 shorter events, 71.7 us)
Async XLA Ops:
  7.2 293.3 %reduce-scatter.2.cloned.1.call-start = ((), (), s32[]{:S(2)}) async-start(), calls=%async_computation.1 | async-start | bytes 2621440 | tf_op jit(solution)/shard_map/reduce_scatter | solution.py:98
  9.5 50.8 %collective-permute-start = (f32[4,64,512]{2,1,0:T(8,128)}, f32[4,64,512]{2,1,0:T(8,128)}, u32[]{:S(2)}, u32[]{:S(2)}) collective-permute-start(f32[4,64,512]{2,1,0:T(8,128)} %get-tuple-element.58), channel_id=1, source_target_pairs={{1,0},{2,1},{3,2},{4,3},{5,4},{6,5},{7,6},{9,8},{10,9},{11,10},{12... | collective-permute-start | bytes 1572872 | tf_op jit(solution)/shard_map/ppermute | solution.py:20
  10.8 49.5 %collective-permute-start.1 = (f32[4,64,512]{2,1,0:T(8,128)}, f32[4,64,512]{2,1,0:T(8,128)}, u32[]{:S(2)}, u32[]{:S(2)}) collective-permute-start(f32[4,64,512]{2,1,0:T(8,128)} %get-tuple-element.59), channel_id=1, source_target_pairs={{0,1},{1,2},{2,3},{3,4},{4,5},{5,6},{6,7},{8,9},{9,10},{10,11},{11... | collective-permute-start | bytes 1572872 | tf_op jit(solution)/shard_map/ppermute | solution.py:17
  17.1 3.3 %copy-start.11 = (s32[1,6,16,64,128]{4,3,2,1,0:T(8,128)S(1)}, s32[1,6,16,64,128]{4,3,2,1,0:T(8,128)}, u32[]{:S(2)}) copy-start(s32[1,6,16,64,128]{4,3,2,1,0:T(8,128)} %param.14) | copy-start | bytes 9437188
  20.4 3.7 %copy-start.24 = (s32[1,256]{1,0:T(1,128)S(1)}, s32[1,256]{1,0:T(1,128)}, u32[]{:S(2)}) copy-start(s32[1,256]{1,0:T(1,128)} %param.17) | copy-start | bytes 3076
  20.4 3.7 %copy-start.21 = (s32[1,6,16,256]{3,2,1,0:T(8,128)S(1)}, s32[1,6,16,256]{3,2,1,0:T(8,128)}, u32[]{:S(2)}) copy-start(s32[1,6,16,256]{3,2,1,0:T(8,128)} %param.15) | copy-start | bytes 294916
  20.4 3.8 %copy-start.25 = (f32[64]{0:T(128)S(1)}, f32[64]{0:T(128)}, u32[]{:S(2)}) copy-start(f32[64]{0:T(128)} %param.16) | copy-start | bytes 772
  33.1 2.8 copy-start.12
  33.1 2.8 copy-start.13
  33.1 2.8 copy-start.14
  38.6 9.6 %copy-start.10 = (f32[16,64,4,128]{3,1,0,2:T(8,128)}, f32[16,64,4,128]{3,1,0,2:T(8,128)S(1)}, u32[]{:S(2)}) copy-start(f32[16,64,4,128]{3,1,0,2:T(8,128)S(1)} %get-tuple-element.83) | copy-start | bytes 6291460
  51.7 8.0 %copy-start.23 = (f32[1,4,256]{2,1,0:T(4,128)S(1)}, f32[1,4,256]{2,1,0:T(4,128)}, u32[]{:S(2)}) copy-start(f32[1,4,256]{2,1,0:T(4,128)} %param.18) | copy-start | bytes 12292
  51.7 8.6 %copy-start.2 = (f32[16,64,512]{2,1,0:T(8,128)S(1)}, f32[16,64,512]{2,1,0:T(8,128)}, u32[]{:S(2)}) copy-start(f32[16,64,512]{2,1,0:T(8,128)} %param.13) | copy-start | bytes 6291460
  93.1 9.8 %copy-start.7 = (f32[524288]{0:T(1024)}, f32[524288]{0:T(1024)S(1)}, u32[]{:S(2)}) copy-start(f32[524288]{0:T(1024)S(1)} %scatter_fusion) | copy-start | bytes 6291460
  96.1 26.2 %collective-permute-start.3 = (f32[4,64,512]{2,1,0:T(8,128)}, f32[4,64,512]{2,1,0:T(8,128)}, u32[]{:S(2)}, u32[]{:S(2)}) collective-permute-start(f32[4,64,512]{2,1,0:T(8,128)} %slice.517), channel_id=1, source_target_pairs={{0,1},{1,2},{2,3},{3,4},{4,5},{5,6},{6,7},{8,9},{9,10},{10,11},{11... | collective-permute-start | bytes 1572872 | tf_op jit(solution)/shard_map/ppermute | solution.py:17
  102.9 21.1 %collective-permute-start.2 = (f32[4,64,512]{2,1,0:T(8,128)}, f32[4,64,512]{2,1,0:T(8,128)}, u32[]{:S(2)}, u32[]{:S(2)}) collective-permute-start(f32[4,64,512]{2,1,0:T(8,128)} %slice.514), channel_id=1, source_target_pairs={{1,0},{2,1},{3,2},{4,3},{5,4},{6,5},{7,6},{9,8},{10,9},{11,10},{12... | collective-permute-start | bytes 1572872 | tf_op jit(solution)/shard_map/ppermute | solution.py:20
  137.3 9.7 %copy-start.22 = (s32[1,3]{1,0:T(1,128)S(1)}, s32[1,3]{1,0:T(1,128)}, u32[]{:S(2)}) copy-start(s32[1,3]{1,0:T(1,128)} %param.19) | copy-start | bytes 40
  141.5 25.7 %collective-permute-start.5 = (f32[4,64,512]{2,1,0:T(8,128)}, f32[4,64,512]{2,1,0:T(8,128)}, u32[]{:S(2)}, u32[]{:S(2)}) collective-permute-start(f32[4,64,512]{2,1,0:T(8,128)} %slice.548), channel_id=1, source_target_pairs={{0,1},{1,2},{2,3},{3,4},{4,5},{5,6},{6,7},{8,9},{9,10},{10,11},{11... | collective-permute-start | bytes 1572872 | tf_op jit(solution)/shard_map/ppermute | solution.py:17
  150.3 20.3 %collective-permute-start.4 = (f32[4,64,512]{2,1,0:T(8,128)}, f32[4,64,512]{2,1,0:T(8,128)}, u32[]{:S(2)}, u32[]{:S(2)}) collective-permute-start(f32[4,64,512]{2,1,0:T(8,128)} %slice.545), channel_id=1, source_target_pairs={{1,0},{2,1},{3,2},{4,3},{5,4},{6,5},{7,6},{9,8},{10,9},{11,10},{12... | collective-permute-start | bytes 1572872 | tf_op jit(solution)/shard_map/ppermute | solution.py:20
  168.2 3.4 %copy-start = (f32[16,64,512]{2,1,0:T(8,128)S(1)}, f32[16,64,512]{2,1,0:T(8,128)}, u32[]{:S(2)}) copy-start(f32[16,64,512]{2,1,0:T(8,128)} %reshape.605) | copy-start | bytes 6291460
  168.2 3.4 %copy-start.4 = (f32[16,64,512]{2,1,0:T(8,128)S(1)}, f32[16,64,512]{2,1,0:T(8,128)}, u32[]{:S(2)}) copy-start(f32[16,64,512]{2,1,0:T(8,128)} %param.13) | copy-start | bytes 6291460
  187.4 13.6 %collective-permute-start.7 = (f32[4,64,512]{2,1,0:T(8,128)}, f32[4,64,512]{2,1,0:T(8,128)}, u32[]{:S(2)}, u32[]{:S(2)}) collective-permute-start(f32[4,64,512]{2,1,0:T(8,128)} %slice.582), channel_id=1, source_target_pairs={{0,1},{1,2},{2,3},{3,4},{4,5},{5,6},{6,7},{8,9},{9,10},{10,11},{11... | collective-permute-start | bytes 1572872 | tf_op jit(solution)/shard_map/ppermute | solution.py:17
  214.4 54.2 %collective-permute-start.6 = (f32[4,64,512]{2,1,0:T(8,128)S(1)}, f32[4,64,512]{2,1,0:T(8,128)S(1)}, u32[]{:S(2)}, u32[]{:S(2)}) collective-permute-start(f32[4,64,512]{2,1,0:T(8,128)S(1)} %slice.579), channel_id=1, source_target_pairs={{1,0},{2,1},{3,2},{4,3},{5,4},{6,5},{7,6},{9,8},{10,9},{11,10},{12... | collective-permute-start | bytes 1572872 | tf_op jit(solution)/shard_map/ppermute | solution.py:20
  265.6 3.7 %copy-start.1 = (f32[16,64,512]{2,1,0:T(8,128)S(1)}, f32[16,64,512]{2,1,0:T(8,128)}, u32[]{:S(2)}) copy-start(f32[16,64,512]{2,1,0:T(8,128)} %reshape.605) | copy-start | bytes 6291460
  (11 other events, 26.3 us)
Sparse Core Ops, SparseCore 0:
  213.4 33.5 reduce-scatter.1
where the time goes:
time: 310 us; the launch traced here: 308 us
  other arithmetic  113 us (36%)
  local copies, waits for them, and re-layouts  74.6 us (24%)
  blocking collectives  46.7 us (15%)
  waiting for transfers between devices  28.4 us (9%)
  starting transfers between devices  26.9 us (9%)
  between operations  18.8 us (6%)
    add x4, other arithmetic, body(): stepped = 2.0 * now - later + courant * laplace(now)  65.4 us
    psum x1, blocking collectives, body(): misfit = 0.5 * lax.psum(misfit_part, ('shot', 'space')) / count  46.7 us
    ppermute x4, waiting for transfers between devices, with_halo(): lax.ppermute(lax.slice_in_dim(block, block.shape[dim] - width, None, axis...  28.4 us
    ppermute x4, starting transfers between devices, with_halo(): lax.ppermute(lax.slice_in_dim(block, block.shape[dim] - width, None, axis...  21.5 us
    scatter-add x4, other arithmetic, body(): stepped.reshape(-1).at[cells].add(residual).reshape(depth, rows, cols)  15.3 us
    unnamed x2, other arithmetic  14.8 us
    unnamed x61, local copies, waits for them, and re-layouts  13.9 us
    gather x4, local copies, waits for them, and re-layouts, body(): synthetic = jnp.take(fields[level].reshape(-1), cells)  13.8 us
  transfers between devices with their start and end apart: 9, of which 3 were waited for; matrix products, arithmetic and copies ran while one was open for 33% of the time, Pallas kernels for 0%

commit v1 on v0

--- a/solution.py
+++ b/solution.py
@@ -97,7 +97,7 @@
     muted = image * (1.0 - jnp.exp(-dist / (2.0 * MUTE * MUTE)))
     gradient = lax.psum_scatter(muted, "shot", scatter_dimension=1, tiled=True)
     count = lax.axis_size("shot") * ITERS * receiver_cell.shape[1] * lax.axis_size("space")
-    misfit = 0.5 * lax.psum(misfit_part, ("shot", "space")) / count
+    misfit = 0.5 * jnp.sum(lax.all_gather(misfit_part, ("shot", "space")), axis=0) / count
     return (gradient, now[None], later[None], misfit)
 
 

time: 310 us -> 310 us (level)
    psum x1 -> x0, blocking collectives: 46.7 us -> none  [body(): misfit = 0.5 * lax.psum(misfit_part, ('shot', 'space')) / count]
    unnamed x0 -> x1, blocking collectives: none -> 46.5 us
    unnamed x61 -> x63, local copies, waits for them, and re-layouts: 13.9 us -> 14.3 us
where the time goes in v1:
time: 310 us; the launch traced here: 308 us
  other arithmetic  113 us (36%)
  local copies, waits for them, and re-layouts  75 us (24%)
  blocking collectives  46.5 us (15%)
  waiting for transfers between devices  28.4 us (9%)
  starting transfers between devices  26.7 us (9%)
  between operations  18.8 us (6%)
    add x4, other arithmetic, body(): stepped = 2.0 * now - later + courant * laplace(now)  65.4 us
    unnamed x1, blocking collectives  46.5 us
    ppermute x4, waiting for transfers between devices, with_halo(): lax.ppermute(lax.slice_in_dim(block, block.shape[dim] - width, None, axis...  28.4 us
    ppermute x4, starting transfers between devices, with_halo(): lax.ppermute(lax.slice_in_dim(block, block.shape[dim] - width, None, axis...  21.5 us
    scatter-add x4, other arithmetic, body(): stepped.reshape(-1).at[cells].add(residual).reshape(depth, rows, cols)  15.3 us
    unnamed x2, other arithmetic  14.7 us
    unnamed x63, local copies, waits for them, and re-layouts  14.3 us
    gather x4, local copies, waits for them, and re-layouts, body(): synthetic = jnp.take(fields[level].reshape(-1), cells)  13.8 us
  transfers between devices with their start and end apart: 9, of which 3 were waited for; matrix products, arithmetic and copies ran while one was open for 33% of the time, Pallas kernels for 0%

profile of v1, /device:TPU:0, one launch (start us, length us, event | category | flops | bytes accessed | tf_op | source)
XLA Modules:
  0.0 308.0 jit_solution(12524703564216571912)
XLA Ops:
  10.8 6.3 %collective-permute-start.1 = (f32[4,64,512]{2,1,0:T(8,128)}, f32[4,64,512]{2,1,0:T(8,128)}, u32[]{:S(2)}, u32[]{:S(2)}) collective-permute-start(f32[4,64,512]{2,1,0:T(8,128)} %get-tuple-element.59), channel_id=1, source_target_pairs={{0,1},{1,2},{2,3},{3,4},{4,5},{5,6},{6,7},{8,9},{9,10},{10,11},{11... | collective-permute-start | bytes 1572872 | tf_op jit(solution)/shard_map/ppermute | solution.py:17
  17.1 3.1 %and_bitcast_fusion.7 = (s32[16,64,1,128]{3,1,0,2:T(8,128)}, s32[16,64,1,128]{3,1,0,2:T(8,128)}, s32[16,64,1,128]{3,1,0,2:T(8,128)S(1)}, s32[16,64,1,128]{3,1,0,2:T(8,128)S(1)}, s32[16,64,1,128]{3,1,0,2:T(8,128)S(1)}) fusion(s32[1,6,16,64,128]{4,3,2,1,0:T(8,128)} %param.14), kind=kLoop, calls=%fused_computation.304 | loop fusion | flops 1310720 | bytes 5242880 | tf_op jit(solution)/shard_map/and | solution.py:26
  20.2 3.4 %and_bitcast_fusion.23 = (s32[16,64,1,128]{3,1,0,2:T(8,128)S(1)}, s32[16,64,1,128]{3,1,0,2:T(8,128)}, s32[16,64,1,128]{3,1,0,2:T(8,128)}, s32[16,64,1,128]{3,1,0...) fusion(s32[1,6,16,64,128]{4,3,2,1,0:T(8,128)S(1)} %copy-done.11), kind=kLoop, calls=%fused_computation.322 | loop fusion | flops 4980736 | bytes 13107200 | tf_op jit(solution)/shard_map/and | solution.py:26
  25.9 3.4 %fusion.162 = (f32[16,64,4,128]{3,1,0,2:T(8,128)S(1)}, f32[16,64,4,128]{3,1,0,2:T(8,128)S(1)}) fusion(s32[16,64,1,128]{3,1,0,2:T(8,128)} %get-tuple-element.27, s32[16,64,1,128]{3,1,0,2:T(8,128)S(1)} %get-tuple-element.26, s32[16,64,1,128]{3,1,0,2:T(8,128)S(1)} %get-tuple-element.25, s32[16,64,1,128]{3,1,0,2:T(8,128)S(1)} %get-tuple-element.43, ...), kind=kLoop, calls=%fused_computation.270 | loop fusion | flops 6291456 | bytes 8421376 | tf_op jit(solution)/shard_map/mul | solution.py:32
  37.6 3.4 %gather_fusion = f32[256]{0:T(256)S(1)} fusion(f32[524288]{0:T(1024)} %bitcast.182, s32[1024]{0:T(1024)S(1)} %pad_clamp_fusion), kind=kCustom, calls=%fused_computation.clone | custom fusion | bytes 3072 | tf_op jit(solution)/shard_map/jit(_take)/gather | solution.py:82
  41.0 3.5 %gather_fusion.1 = f32[256]{0:T(256)S(1)} fusion(f32[524288]{0:T(1024)} %bitcast.183, s32[1024]{0:T(1024)S(1)} %pad_clamp_fusion), kind=kCustom, calls=%fused_computation.1.clone | custom fusion | bytes 3072 | tf_op jit(solution)/shard_map/jit(_take)/gather | solution.py:82
  47.2 3.5 %gather_fusion.2 = f32[256]{0:T(256)S(1)} fusion(f32[524288]{0:T(1024)} %bitcast.185, s32[1024]{0:T(1024)S(1)} %pad_clamp_fusion), kind=kCustom, calls=%fused_computation.2.clone | custom fusion | bytes 3072 | tf_op jit(solution)/shard_map/jit(_take)/gather | solution.py:82
  50.7 4.5 %copy.51 = f32[16,64,4,128]{3,2,1,0:T(4,128)} copy(f32[16,64,4,128]{3,1,0,2:T(8,128)} %get-tuple-element.84) | data formatting | bytes 4194304 | tf_op jit(solution)/shard_map/mul | solution.py:32
  55.2 3.5 %gather_fusion.3 = f32[256]{0:T(256)S(1)} fusion(f32[524288]{0:T(1024)} %bitcast.184, s32[1024]{0:T(1024)S(1)} %pad_clamp_fusion), kind=kCustom, calls=%fused_computation.3.clone | custom fusion | bytes 3072 | tf_op jit(solution)/shard_map/jit(_take)/gather | solution.py:82
  59.4 29.2 %fusion.10 = f32[16,64,512]{2,1,0:T(8,128)S(1)} fusion(f32[16,64,512]{2,1,0:T(8,128)S(1)} %copy-done.2, f32[16,64,512]{2,1,0:T(8,128)} %bitcast.174, f32[4,64,512]{2,1,0:T(8,128)} %collective-permute-done.1, f32[4,64,512]{2,1,0:T(8,128)} %collective-permute-done, f32[1,16,64,512]{3,2,1,0:T(8,128)} %param.12), kind=kLoop, calls=%fused_computation.94 | loop fusion | flops 25690112 | bytes 9437184 | tf_op jit(solution)/shard_map/add | solution.py:86
  89.2 2.9 scatter_fusion
  95.2 4.8 %collective-permute-start.3 = (f32[4,64,512]{2,1,0:T(8,128)}, f32[4,64,512]{2,1,0:T(8,128)}, u32[]{:S(2)}, u32[]{:S(2)}) collective-permute-start(f32[4,64,512]{2,1,0:T(8,128)} %slice.517), channel_id=1, source_target_pairs={{0,1},{1,2},{2,3},{3,4},{4,5},{5,6},{6,7},{8,9},{9,10},{10,11},{11... | collective-permute-start | bytes 1572872 | tf_op jit(solution)/shard_map/ppermute | solution.py:17
  105.0 16.4 %collective-permute-done.3 = f32[4,64,512]{2,1,0:T(8,128)} collective-permute-done((f32[4,64,512]{2,1,0:T(8,128)}, f32[4,64,512]{2,1,0:T(8,128)}, u32[]{:S(2)}, u32[]{:S(2)}) %collective-permute-start.3) | collective-permute-done | bytes 524320 | tf_op jit(solution)/shard_map/ppermute | solution.py:17
  124.8 4.9 %fusion.56 = f32[16,64,512]{2,1,0:T(8,128)S(1)} fusion(f32[16,64,512]{2,1,0:T(8,128)S(1)} %copy-done.3, f32[16,64,512]{2,1,0:T(8,128)S(1)} %reshape.603, f32[20,64,512]{2,1,0:T(8,128)S(1)} %get-tuple-element.57, f32[20,64,512]{2,1,0:T(8,128)S(1)} %constant_dynamic-update-slice_fusion, f32[1,16,64,512]{3,2,1,0:T(8,128)S(1)} %copy-done.6), kind=kLoop, calls=%fused_computation.140 | loop fusion | flops 21495808 | bytes 25165824 | tf_op jit(solution)/shard_map/add | solution.py:86
  131.6 4.8 %scatter_fusion.1 = f32[524288]{0:T(1024)} fusion(f32[524288]{0:T(1024)} %bitcast.176, s32[256]{0:T(256)S(1)} %bitcast.193, f32[256]{0:T(256)S(1)} %get-tuple-element.71), kind=kCustom, calls=%fused_computation.5 | custom fusion | flops 256 | bytes 4096 | tf_op jit(solution)/shard_map/scatter-add | solution.py:87
  140.5 5.2 %collective-permute-start.5 = (f32[4,64,512]{2,1,0:T(8,128)}, f32[4,64,512]{2,1,0:T(8,128)}, u32[]{:S(2)}, u32[]{:S(2)}) collective-permute-start(f32[4,64,512]{2,1,0:T(8,128)} %slice.548), channel_id=1, source_target_pairs={{0,1},{1,2},{2,3},{3,4},{4,5},{5,6},{6,7},{8,9},{9,10},{10,11},{11... | collective-permute-start | bytes 1572872 | tf_op jit(solution)/shard_map/ppermute | solution.py:17
  154.6 11.6 %collective-permute-done.5 = f32[4,64,512]{2,1,0:T(8,128)} collective-permute-done((f32[4,64,512]{2,1,0:T(8,128)}, f32[4,64,512]{2,1,0:T(8,128)}, u32[]{:S(2)}, u32[]{:S(2)}) %collective-permute-start.5) | collective-permute-done | bytes 524320 | tf_op jit(solution)/shard_map/ppermute | solution.py:17
  170.7 5.0 %fusion.85 = f32[16,64,512]{2,1,0:T(8,128)S(1)} fusion(f32[16,64,512]{2,1,0:T(8,128)S(1)} %copy-done.4, f32[16,64,512]{2,1,0:T(8,128)S(1)} %copy-done, f32[20,64,512]{2,1,0:T(8,128)S(1)} %get-tuple-element.53, f32[20,64,512]{2,1,0:T(8,128)S(1)} %constant_dynamic-update-slice_fusion.4, f32[16,64,512]{2,1,0:T(8,128)S(1)} %reshape.603), kind=kLoop, calls=%fused_computation.169 | loop fusion | flops 21495808 | bytes 25165824 | tf_op jit(solution)/shard_map/add | solution.py:86
  177.6 4.8 %scatter_fusion.2 = f32[524288]{0:T(1024)} fusion(f32[524288]{0:T(1024)} %bitcast.173, s32[256]{0:T(256)S(1)} %bitcast.194, f32[256]{0:T(256)S(1)} %get-tuple-element.73), kind=kCustom, calls=%fused_computation.6 | custom fusion | flops 256 | bytes 4096 | tf_op jit(solution)/shard_map/scatter-add | solution.py:87
  186.5 5.2 %collective-permute-start.7 = (f32[4,64,512]{2,1,0:T(8,128)}, f32[4,64,512]{2,1,0:T(8,128)}, u32[]{:S(2)}, u32[]{:S(2)}) collective-permute-start(f32[4,64,512]{2,1,0:T(8,128)} %slice.582), channel_id=1, source_target_pairs={{0,1},{1,2},{2,3},{3,4},{4,5},{5,6},{6,7},{8,9},{9,10},{10,11},{11... | collective-permute-start | bytes 1572872 | tf_op jit(solution)/shard_map/ppermute | solution.py:17
  191.7 5.2 %fusion.160 = (f32[4,16,8,8,128]{4,3,2,1,0:T(8,128)}, f32[4,16,8,8,128]{4,3,2,1,0:T(8,128)}) fusion(s32[16,64,1,128]{3,1,0,2:T(8,128)} %get-tuple-element.24, s32[16,64,1,128]{3,1,0,2:T(8,128)} %get-tuple-element.23, s32[16,64,1,128]{3,1,0,2:T(8,128)} %get-tuple-element.22, s32[16,64,1,128]{3,1,0,2:T(8,128)S(1)} %get-tuple-element.21, ...), kind=kLoop, calls=%fused_computation.267 | loop fusion | flops 6291456 | bytes 8421376
  201.2 9.5 %constant_dynamic-update-slice_fusion.9 = (f32[20,64,512]{2,1,0:T(8,128)}, f32[20,64,512]{2,1,0:T(8,128)S(1)}, f32[16,64,512]{2,1,0:T(8,128)}) fusion(f32[16,64,512]{2,1,0:T(8,128)} %reshape.607, f32[20,64,512]{2,1,0:T(8,128)S(1)} %constant_dynamic-update-slice_fusion.11, s32[512]{0:T(512)S(1)} %subtract_multiply_fusion, ...), kind=kLoop, calls=%fused_computation.332 | loop fusion | flops 13107199 | bytes 27273216
  217.5 46.5 %all-reduce.4 = f32[32]{0:T(128)S(1)} all-reduce(f32[32]{0:T(128)S(1)} %dynamic-update-slice), channel_id=1, replica_groups=mesh['shot'=4,'space'=8] {'shot','space'}, use_global_device_ids=true, to_apply=%add.4 | all-reduce | flops 32 | bytes 256
  269.0 26.3 %fusion.114 = f32[16,64,512]{2,1,0:T(8,128)S(1)} fusion(f32[16,64,512]{2,1,0:T(8,128)} %param.13, f32[16,64,512]{2,1,0:T(8,128)} %reshape.607, f32[20,64,512]{2,1,0:T(8,128)} %copy-done.5, f32[20,64,512]{2,1,0:T(8,128)} %constant_dynamic-update-slice_fusion.8, f32[16,64,512]{2,1,0:T(8,128)S(1)} %copy-done.1), kind=kLoop, calls=%fused_computation.198 | loop fusion | flops 21495808 | bytes 25165824 | tf_op jit(solution)/shard_map/add | solution.py:86
  (124 shorter events, 72.3 us)
Async XLA Ops:
  7.2 292.9 %reduce-scatter.2.cloned.1.call-start = ((), (), s32[]{:S(2)}) async-start(), calls=%async_computation.1 | async-start | bytes 2621440 | tf_op jit(solution)/shard_map/reduce_scatter | solution.py:98
  9.5 49.9 %collective-permute-start = (f32[4,64,512]{2,1,0:T(8,128)}, f32[4,64,512]{2,1,0:T(8,128)}, u32[]{:S(2)}, u32[]{:S(2)}) collective-permute-start(f32[4,64,512]{2,1,0:T(8,128)} %get-tuple-element.58), channel_id=1, source_target_pairs={{1,0},{2,1},{3,2},{4,3},{5,4},{6,5},{7,6},{9,8},{10,9},{11,10},{12... | collective-permute-start | bytes 1572872 | tf_op jit(solution)/shard_map/ppermute | solution.py:20
  10.8 48.6 %collective-permute-start.1 = (f32[4,64,512]{2,1,0:T(8,128)}, f32[4,64,512]{2,1,0:T(8,128)}, u32[]{:S(2)}, u32[]{:S(2)}) collective-permute-start(f32[4,64,512]{2,1,0:T(8,128)} %get-tuple-element.59), channel_id=1, source_target_pairs={{0,1},{1,2},{2,3},{3,4},{4,5},{5,6},{6,7},{8,9},{9,10},{10,11},{11... | collective-permute-start | bytes 1572872 | tf_op jit(solution)/shard_map/ppermute | solution.py:17
  17.1 3.1 %copy-start.11 = (s32[1,6,16,64,128]{4,3,2,1,0:T(8,128)S(1)}, s32[1,6,16,64,128]{4,3,2,1,0:T(8,128)}, u32[]{:S(2)}) copy-start(s32[1,6,16,64,128]{4,3,2,1,0:T(8,128)} %param.14) | copy-start | bytes 9437188
  20.2 3.4 %copy-start.24 = (s32[1,256]{1,0:T(1,128)S(1)}, s32[1,256]{1,0:T(1,128)}, u32[]{:S(2)}) copy-start(s32[1,256]{1,0:T(1,128)} %param.17) | copy-start | bytes 3076
  20.2 3.4 %copy-start.21 = (s32[1,6,16,256]{3,2,1,0:T(8,128)S(1)}, s32[1,6,16,256]{3,2,1,0:T(8,128)}, u32[]{:S(2)}) copy-start(s32[1,6,16,256]{3,2,1,0:T(8,128)} %param.15) | copy-start | bytes 294916
  20.2 3.4 %copy-start.25 = (f32[64]{0:T(128)S(1)}, f32[64]{0:T(128)}, u32[]{:S(2)}) copy-start(f32[64]{0:T(128)} %param.16) | copy-start | bytes 772
  32.1 2.8 copy-start.12
  32.1 2.8 copy-start.13
  32.1 2.8 copy-start.14
  37.6 9.6 %copy-start.10 = (f32[16,64,4,128]{3,1,0,2:T(8,128)}, f32[16,64,4,128]{3,1,0,2:T(8,128)S(1)}, u32[]{:S(2)}) copy-start(f32[16,64,4,128]{3,1,0,2:T(8,128)S(1)} %get-tuple-element.83) | copy-start | bytes 6291460
  50.7 8.0 %copy-start.23 = (f32[1,4,256]{2,1,0:T(4,128)S(1)}, f32[1,4,256]{2,1,0:T(4,128)}, u32[]{:S(2)}) copy-start(f32[1,4,256]{2,1,0:T(4,128)} %param.18) | copy-start | bytes 12292
  50.7 8.7 %copy-start.2 = (f32[16,64,512]{2,1,0:T(8,128)S(1)}, f32[16,64,512]{2,1,0:T(8,128)}, u32[]{:S(2)}) copy-start(f32[16,64,512]{2,1,0:T(8,128)} %param.13) | copy-start | bytes 6291460
  92.1 9.8 %copy-start.7 = (f32[524288]{0:T(1024)}, f32[524288]{0:T(1024)S(1)}, u32[]{:S(2)}) copy-start(f32[524288]{0:T(1024)S(1)} %scatter_fusion) | copy-start | bytes 6291460
  95.2 26.2 %collective-permute-start.3 = (f32[4,64,512]{2,1,0:T(8,128)}, f32[4,64,512]{2,1,0:T(8,128)}, u32[]{:S(2)}, u32[]{:S(2)}) collective-permute-start(f32[4,64,512]{2,1,0:T(8,128)} %slice.517), channel_id=1, source_target_pairs={{0,1},{1,2},{2,3},{3,4},{4,5},{5,6},{6,7},{8,9},{9,10},{10,11},{11... | collective-permute-start | bytes 1572872 | tf_op jit(solution)/shard_map/ppermute | solution.py:17
  102.0 21.1 %collective-permute-start.2 = (f32[4,64,512]{2,1,0:T(8,128)}, f32[4,64,512]{2,1,0:T(8,128)}, u32[]{:S(2)}, u32[]{:S(2)}) collective-permute-start(f32[4,64,512]{2,1,0:T(8,128)} %slice.514), channel_id=1, source_target_pairs={{1,0},{2,1},{3,2},{4,3},{5,4},{6,5},{7,6},{9,8},{10,9},{11,10},{12... | collective-permute-start | bytes 1572872 | tf_op jit(solution)/shard_map/ppermute | solution.py:20
  136.4 9.7 %copy-start.22 = (s32[1,3]{1,0:T(1,128)S(1)}, s32[1,3]{1,0:T(1,128)}, u32[]{:S(2)}) copy-start(s32[1,3]{1,0:T(1,128)} %param.19) | copy-start | bytes 40
  140.5 25.7 %collective-permute-start.5 = (f32[4,64,512]{2,1,0:T(8,128)}, f32[4,64,512]{2,1,0:T(8,128)}, u32[]{:S(2)}, u32[]{:S(2)}) collective-permute-start(f32[4,64,512]{2,1,0:T(8,128)} %slice.548), channel_id=1, source_target_pairs={{0,1},{1,2},{2,3},{3,4},{4,5},{5,6},{6,7},{8,9},{9,10},{10,11},{11... | collective-permute-start | bytes 1572872 | tf_op jit(solution)/shard_map/ppermute | solution.py:17
  149.4 20.2 %collective-permute-start.4 = (f32[4,64,512]{2,1,0:T(8,128)}, f32[4,64,512]{2,1,0:T(8,128)}, u32[]{:S(2)}, u32[]{:S(2)}) collective-permute-start(f32[4,64,512]{2,1,0:T(8,128)} %slice.545), channel_id=1, source_target_pairs={{1,0},{2,1},{3,2},{4,3},{5,4},{6,5},{7,6},{9,8},{10,9},{11,10},{12... | collective-permute-start | bytes 1572872 | tf_op jit(solution)/shard_map/ppermute | solution.py:20
  167.3 3.4 %copy-start = (f32[16,64,512]{2,1,0:T(8,128)S(1)}, f32[16,64,512]{2,1,0:T(8,128)}, u32[]{:S(2)}) copy-start(f32[16,64,512]{2,1,0:T(8,128)} %reshape.605) | copy-start | bytes 6291460
  167.3 3.4 %copy-start.4 = (f32[16,64,512]{2,1,0:T(8,128)S(1)}, f32[16,64,512]{2,1,0:T(8,128)}, u32[]{:S(2)}) copy-start(f32[16,64,512]{2,1,0:T(8,128)} %param.13) | copy-start | bytes 6291460
  186.5 13.6 %collective-permute-start.7 = (f32[4,64,512]{2,1,0:T(8,128)}, f32[4,64,512]{2,1,0:T(8,128)}, u32[]{:S(2)}, u32[]{:S(2)}) collective-permute-start(f32[4,64,512]{2,1,0:T(8,128)} %slice.582), channel_id=1, source_target_pairs={{0,1},{1,2},{2,3},{3,4},{4,5},{5,6},{6,7},{8,9},{9,10},{10,11},{11... | collective-permute-start | bytes 1572872 | tf_op jit(solution)/shard_map/ppermute | solution.py:17
  213.3 54.8 %collective-permute-start.6 = (f32[4,64,512]{2,1,0:T(8,128)S(1)}, f32[4,64,512]{2,1,0:T(8,128)S(1)}, u32[]{:S(2)}, u32[]{:S(2)}) collective-permute-start(f32[4,64,512]{2,1,0:T(8,128)S(1)} %slice.579), channel_id=1, source_target_pairs={{1,0},{2,1},{3,2},{4,3},{5,4},{6,5},{7,6},{9,8},{10,9},{11,10},{12... | collective-permute-start | bytes 1572872 | tf_op jit(solution)/shard_map/ppermute | solution.py:20
  265.2 3.7 %copy-start.1 = (f32[16,64,512]{2,1,0:T(8,128)S(1)}, f32[16,64,512]{2,1,0:T(8,128)}, u32[]{:S(2)}) copy-start(f32[16,64,512]{2,1,0:T(8,128)} %reshape.605) | copy-start | bytes 6291460
  (11 other events, 26.3 us)
Sparse Core Ops, SparseCore 0:
  212.4 33.5 reduce-scatter.1
